TPU v7x, 32 devices: a whole 2x2x4 slice. The times are simulated.
32 devices in a mesh: sub: 8 (over z, y), dom: 4 (over x, core).
Axes of the slice: x: 2, y: 2, z: 4, core: 2. Of those that a mesh axis runs over, the one named last changes fastest.
Arguments:
- source_points: float32 [128, 3, 4096], P(('sub', 'dom')), may hold values from -4 to 4
- boundary: float32 [128, 8, 6, 128], P(('sub', 'dom')), may hold values from -4 to 4, as said below
- poses: float32 [12, 128], replicated, may hold values from -2 to 2, as said below
- anchor: float32 [128], P(('sub', 'dom')), may hold values from 0.3 to 3
- edge_target: int32 [128, 4], P(('sub', 'dom')), may hold values from 0 to 47, as said below
- corr_tile: int32 [128, 4, 4], P(('sub', 'dom')), may hold values from 0 to 7
- corr_source: int32 [128, 4, 4, 128], P(('sub', 'dom')), may hold values from 0 to 4095
- corr_lane: int32 [128, 4, 4, 128], P(('sub', 'dom')), may hold values from 0 to 127
Outputs:
- refined_pose: float32 [12, 128], P(None, ('sub', 'dom'))
Inputs may be any that keep to these rules, and one draw needn't show every extreme that they name: `poses`: each column holds a rotation matrix, row-major, followed by a translation. `boundary`: in every column of 6 entries the last 3 form a unit vector. `edge_target`: entry v of scan s names scan v % 16 of the previous (v // 16 = 0), the same (1) or the next (2) submap along the closed chain of submaps; it never names s itself; one scan may be named by several edges of s.
All inputs are finite; a program needn't handle non-finite values.
Results may differ from a plain program's by a relative error of at most 0.0001.
Values sent between devices are 32-bit elements; how exact they have to be, the bound alone decides.
No kernel may reach another device: no remote copies, remote signals or barrier semaphores. Data moves between devices by JAX's collectives and lax.ppermute only.
A program may use at most 64 MiB of HBM per device.

v0:
```python
import jax
import jax.numpy as jnp
from jax import lax
from jax.sharding import PartitionSpec as P

CG_ITERS = 2
GN_ITERS = 2
FINEST = lax.Precision.HIGHEST


def from_behind(block, axis, distance):
    devices = range(lax.axis_size(axis))
    route = [((i - distance) % len(devices), i) for i in devices]
    return lax.ppermute(block, axis, route)


def cayley(vector):
    first, second, third = (vector[0], vector[1], vector[2])
    length_sq = first * first + second * second + third * third
    inverse = 1.0 / (1.0 + length_sq)
    trace_part = 1.0 - length_sq
    entries = [
        [
            trace_part + 2.0 * first * first,
            2.0 * first * second - 2.0 * third,
            2.0 * first * third + 2.0 * second,
        ],
        [
            2.0 * first * second + 2.0 * third,
            trace_part + 2.0 * second * second,
            2.0 * second * third - 2.0 * first,
        ],
        [
            2.0 * first * third - 2.0 * second,
            2.0 * second * third + 2.0 * first,
            trace_part + 2.0 * third * third,
        ],
    ]
    return jnp.stack([jnp.stack(line) for line in entries]) * inverse


def rotate(matrix, vector):
    return jnp.stack(
        [
            matrix[row_id, 0] * vector[0]
            + matrix[row_id, 1] * vector[1]
            + matrix[row_id, 2] * vector[2]
            for row_id in range(3)
        ]
    )


def update(pose, increment):
    rotation = pose[:9].reshape(3, 3, -1)
    turn_mat = cayley(0.5 * increment[:3])
    rotated = jnp.stack(
        [
            jnp.stack(
                [
                    turn_mat[row_id, 0] * rotation[0, col_id]
                    + turn_mat[row_id, 1] * rotation[1, col_id]
                    + turn_mat[row_id, 2] * rotation[2, col_id]
                    for col_id in range(3)
                ]
            )
            for row_id in range(3)
        ]
    )
    moved_to = rotate(turn_mat, pose[9:]) + increment[3:]
    return jnp.concatenate([rotated.reshape(9, -1), moved_to], axis=0)


def scan_terms(points, pose_here, target_tiles, target_pose, sources, lane_ids):
    edge_count = sources.shape[0]
    picked = jnp.take(points, sources, axis=1)
    placed = rotate(pose_here[:9].reshape(3, 3), picked) + pose_here[9:, None, None, None]
    spread_lanes = jnp.broadcast_to(lane_ids[:, :, None, :], target_tiles.shape)
    chosen = jnp.take_along_axis(target_tiles, spread_lanes, axis=3)
    rotation = target_pose[:9].reshape(3, 3, edge_count)[:, :, :, None, None]
    shifted = target_pose[9:, :, None, None]
    target = (
        rotate(rotation, jnp.stack([chosen[:, :, 0], chosen[:, :, 1], chosen[:, :, 2]])) + shifted
    )
    normal = rotate(rotation, jnp.stack([chosen[:, :, 3], chosen[:, :, 4], chosen[:, :, 5]]))
    offset = target - placed
    misfit = normal[0] * offset[0] + normal[1] * offset[1] + normal[2] * offset[2]
    turned = jnp.stack(
        [
            placed[1] * normal[2] - placed[2] * normal[1],
            placed[2] * normal[0] - placed[0] * normal[2],
            placed[0] * normal[1] - placed[1] * normal[0],
        ]
    )
    jacobian = jnp.concatenate([turned, normal], axis=0).reshape(6, edge_count, -1)
    samples = jacobian.shape[2]
    blocks = jnp.einsum("aem,bem->eab", jacobian, jacobian, precision=FINEST) / samples
    slopes = (
        jnp.einsum("aem,em->ea", jacobian, misfit.reshape(edge_count, -1), precision=FINEST)
        / samples
    )
    return (blocks, slopes)


def window_order(sub_index, groups, scan_sub):
    slot_ids = (sub_index + jnp.arange(3, dtype=jnp.int32) - 1) % groups
    return (slot_ids[:, None] * scan_sub + jnp.arange(scan_sub, dtype=jnp.int32)[None, :]).reshape(
        -1
    )


def global_sum(value):
    return lax.psum(value, ("sub", "dom"))


def spread_out(own_part):
    pieces = [from_behind(own_part, "sub", offset_by) for offset_by in (1, -1)]
    before, middle, beyond = (
        lax.all_gather(pieces[0], "dom", axis=1, tiled=True),
        lax.all_gather(own_part, "dom", axis=1, tiled=True),
        lax.all_gather(pieces[1], "dom", axis=1, tiled=True),
    )
    nearby = jnp.concatenate([before, middle, beyond], axis=1)
    return nearby


def collect(partial_value):
    layers = partial_value.shape[0]
    scan_sub = partial_value.shape[2] // 3
    shared = lax.psum_scatter(
        partial_value.reshape(layers, 6, 3, scan_sub), "dom", scatter_dimension=3, tiled=True
    )
    summed = shared[:, :, 1]
    for slot_id, offset_by in ((0, -1), (2, 1)):
        summed = summed + from_behind(shared[:, :, slot_id], "sub", offset_by)
    return summed


def local(source_points, boundary, poses, anchor, edge_target, corr_tile, corr_source, corr_lane):
    scan_dev = source_points.shape[0]
    edge_count = edge_target.shape[1]
    groups = lax.axis_size("sub")
    scan_sub = scan_dev * lax.axis_size("dom")
    sub_index = lax.axis_index("sub")
    dom_index = lax.axis_index("dom")
    window_index = window_order(sub_index, groups, scan_sub)
    middle = lax.all_gather(boundary, "dom", axis=0, tiled=True)
    pieces = [from_behind(middle, "sub", offset_by) for offset_by in (1, -1)]
    window_tiles = jnp.concatenate([pieces[0], middle, pieces[1]], axis=0)
    window_pose = jnp.take(poses, window_index, axis=1)
    own_start = scan_sub + dom_index * scan_dev
    source_at = (own_start + jnp.arange(scan_dev, dtype=jnp.int32))[:, None] + jnp.zeros(
        (1, edge_count), jnp.int32
    )
    from_end = source_at.reshape(-1)
    to_end = edge_target.reshape(-1)
    win_width = 3 * scan_sub
    for turn_id in range(GN_ITERS):
        own_pose = lax.dynamic_slice_in_dim(window_pose, own_start, scan_dev, 1)

        def per_scan(per_item, window_pose=window_pose):
            points, pose_here, targets, tile_ids, sources, lane_ids = per_item
            return scan_terms(
                points,
                pose_here,
                window_tiles[targets[:, None], tile_ids],
                jnp.take(window_pose, targets, axis=1),
                sources,
                lane_ids,
            )

        blocks, slopes = lax.map(
            per_scan, (source_points, own_pose.T, edge_target, corr_tile, corr_source, corr_lane)
        )
        blocks = blocks.reshape(-1, 6, 6)
        slopes = slopes.reshape(-1, 6)
        diag_terms = jnp.diagonal(blocks, axis1=1, axis2=2)
        empty = jnp.zeros((6, win_width), jnp.float32)
        right_part = empty.at[:, from_end].add(slopes.T).at[:, to_end].add(-slopes.T)
        diag_part = empty.at[:, from_end].add(diag_terms.T).at[:, to_end].add(diag_terms.T)
        totals = collect(jnp.stack([right_part, diag_part]))
        right_side = totals[0]
        diagonal_sum = totals[1] + anchor[None, :]

        def apply_system(vector, blocks=blocks):
            nearby = spread_out(vector)
            spread = nearby[:, from_end] - nearby[:, to_end]
            pushed = jnp.einsum("kab,bk->ak", blocks, spread, precision=FINEST)
            partial_value = (
                jnp.zeros((6, win_width), jnp.float32)
                .at[:, from_end]
                .add(pushed)
                .at[:, to_end]
                .add(-pushed)
            )
            return collect(partial_value[None])[0] + anchor[None, :] * vector

        residual = right_side
        scaled = residual / diagonal_sum
        direction = scaled
        energy = global_sum(jnp.sum(residual * scaled))
        increment = jnp.zeros((6, scan_dev), jnp.float32)
        for sweep in range(CG_ITERS):
            image = apply_system(direction)
            step_len = energy / global_sum(jnp.sum(direction * image))
            increment = increment + step_len * direction
            residual = residual - step_len * image
            if sweep + 1 < CG_ITERS:
                scaled = residual / diagonal_sum
                renewed = global_sum(jnp.sum(residual * scaled))
                direction = scaled + renewed / energy * direction
                energy = renewed
        window_pose = update(window_pose, spread_out(increment))
    return lax.dynamic_slice_in_dim(window_pose, own_start, scan_dev, 1)


def solution(mesh):
    in_specs = (
        P(("sub", "dom"), None, None),
        P(("sub", "dom"), None, None, None),
        P(),
        P(("sub", "dom")),
        P(("sub", "dom"), None),
        P(("sub", "dom"), None, None),
        P(("sub", "dom"), None, None, None),
        P(("sub", "dom"), None, None, None),
    )
    out_specs = P(None, ("sub", "dom"))
    return jax.shard_map(local, mesh=mesh, in_specs=in_specs, out_specs=out_specs, check_vma=False)
```

profile of v0, /device:TPU:0, one launch (start us, length us, event | category | flops | bytes accessed | tf_op | source)
XLA Modules:
  0.0 1411.9 jit_solution(11835580075408723627)
XLA Ops:
  0.0 8.3 all_gather.57
  15.1 5.6 copy.252
  31.0 440.6 %while.24 = (s32[]{:T(128)}, f32[4,4,6,6]{3,1,0,2:T(4,128)S(1)}, f32[4,4,6]{2,1,0:T(4,128)S(1)}, f32[4,12]{1,0:T(4,128)S(1)}, f32[4,3,4096]{1,2,0:T(8,128)}, /*i...) while((s32[]{:T(128)}, f32[4,4,6,6]{3,1,0,2:T(4,128)S(1)}, ...), condition=%wide.region_1.5_spmd, body=%wide.region_0.0_spmd.sunk | while | flops 1492314 | bytes 1967897 | solution.py:171
  47.1 91.5 %gather_fusion.1 = f32[12288]{0:T(1024)S(1)} fusion(f32[4,4,6,128]{3,2,1,0:T(8,128)S(1)} %bitcast.1328, s32[12288]{0:T(1024)S(1)} %reshape.2974), kind=kCustom, calls=%fused_computation.2.clone.clone.1 | custom fusion | bytes 294912 | tf_op jit(solution)/shard_map/while/body/eval_jaxpr/jit(take_along_axis)/gather | solution.py:78
  157.2 91.5 %gather_fusion.1 = f32[12288]{0:T(1024)S(1)} fusion(f32[4,4,6,128]{3,2,1,0:T(8,128)S(1)} %bitcast.1328, s32[12288]{0:T(1024)S(1)} %reshape.2974), kind=kCustom, calls=%fused_computation.2.clone.clone.1 | custom fusion | bytes 294912 | tf_op jit(solution)/shard_map/while/body/eval_jaxpr/jit(take_along_axis)/gather | solution.py:78
  267.4 91.5 %gather_fusion.1 = f32[12288]{0:T(1024)S(1)} fusion(f32[4,4,6,128]{3,2,1,0:T(8,128)S(1)} %bitcast.1328, s32[12288]{0:T(1024)S(1)} %reshape.2974), kind=kCustom, calls=%fused_computation.2.clone.clone.1 | custom fusion | bytes 294912 | tf_op jit(solution)/shard_map/while/body/eval_jaxpr/jit(take_along_axis)/gather | solution.py:78
  377.5 91.5 %gather_fusion.1 = f32[12288]{0:T(1024)S(1)} fusion(f32[4,4,6,128]{3,2,1,0:T(8,128)S(1)} %bitcast.1328, s32[12288]{0:T(1024)S(1)} %reshape.2974), kind=kCustom, calls=%fused_computation.2.clone.clone.1 | custom fusion | bytes 294912 | tf_op jit(solution)/shard_map/while/body/eval_jaxpr/jit(take_along_axis)/gather | solution.py:78
  475.1 10.5 all-reduce
  516.1 11.0 all-reduce.1
  537.0 37.1 %all-reduce.7 = (f32[]{:T(128)}, f32[]{:T(128)}) all-reduce(f32[]{:T(128)} %get-tuple-element.259, f32[]{:T(128)} %get-tuple-element.258), channel_id=1, replica_groups=mesh['sub'=8,'dom'=4] {'sub','dom'}, use_global_device_ids=true, to_apply=%region_8.12 | all-reduce | flops 2 | bytes 16 | tf_op jit(solution)/shard_map/psum | solution.py:112
  576.0 42.3 %psum.58 = f32[]{:T(128)} all-reduce(f32[]{:T(128)} %get-tuple-element.341), channel_id=1, replica_groups=mesh['sub'=8,'dom'=4] {'sub','dom'}, use_global_device_ids=true, to_apply=%region_15.19 | all-reduce | flops 1 | bytes 8 | tf_op jit(solution)/shard_map/psum | solution.py:112
  643.1 11.8 all-reduce.2
  662.0 36.9 %psum.59 = f32[]{:T(128)} all-reduce(f32[]{:T(128)} %fusion.120), channel_id=1, replica_groups=mesh['sub'=8,'dom'=4] {'sub','dom'}, use_global_device_ids=true, to_apply=%region_20.24 | all-reduce | flops 1 | bytes 8 | tf_op jit(solution)/shard_map/psum | solution.py:112
  722.0 440.6 %while.25 = (s32[]{:T(128)}, f32[4,4,6,6]{3,1,0,2:T(4,128)S(1)}, f32[4,4,6]{2,1,0:T(4,128)S(1)}, f32[4,12]{1,0:T(4,128)S(1)}, f32[4,3,4096]{1,2,0:T(8,128)}, /*i...) while((s32[]{:T(128)}, f32[4,4,6,6]{3,1,0,2:T(4,128)S(1)}, ...), condition=%wide.region_22.26_spmd, body=%wide.region_21.25_spmd.sunk | while | flops 1492314 | bytes 1967897 | solution.py:171
  738.1 91.5 %gather_fusion.5 = f32[12288]{0:T(1024)S(1)} fusion(f32[4,4,6,128]{3,2,1,0:T(8,128)S(1)} %bitcast.1329, s32[12288]{0:T(1024)S(1)} %reshape.2987), kind=kCustom, calls=%fused_computation.6.clone.clone.1 | custom fusion | bytes 294912 | tf_op jit(solution)/shard_map/while/body/eval_jaxpr/jit(take_along_axis)/gather | solution.py:78
  848.3 91.5 %gather_fusion.5 = f32[12288]{0:T(1024)S(1)} fusion(f32[4,4,6,128]{3,2,1,0:T(8,128)S(1)} %bitcast.1329, s32[12288]{0:T(1024)S(1)} %reshape.2987), kind=kCustom, calls=%fused_computation.6.clone.clone.1 | custom fusion | bytes 294912 | tf_op jit(solution)/shard_map/while/body/eval_jaxpr/jit(take_along_axis)/gather | solution.py:78
  958.4 91.5 %gather_fusion.5 = f32[12288]{0:T(1024)S(1)} fusion(f32[4,4,6,128]{3,2,1,0:T(8,128)S(1)} %bitcast.1329, s32[12288]{0:T(1024)S(1)} %reshape.2987), kind=kCustom, calls=%fused_computation.6.clone.clone.1 | custom fusion | bytes 294912 | tf_op jit(solution)/shard_map/while/body/eval_jaxpr/jit(take_along_axis)/gather | solution.py:78
  1068.6 91.5 %gather_fusion.5 = f32[12288]{0:T(1024)S(1)} fusion(f32[4,4,6,128]{3,2,1,0:T(8,128)S(1)} %bitcast.1329, s32[12288]{0:T(1024)S(1)} %reshape.2987), kind=kCustom, calls=%fused_computation.6.clone.clone.1 | custom fusion | bytes 294912 | tf_op jit(solution)/shard_map/while/body/eval_jaxpr/jit(take_along_axis)/gather | solution.py:78
  1166.2 12.1 all-reduce.3
  1207.9 11.2 all-reduce.4
  1226.3 37.1 %all-reduce.6 = (f32[]{:T(128)}, f32[]{:T(128)}) all-reduce(f32[]{:T(128)} %get-tuple-element.257, f32[]{:T(128)} %get-tuple-element.256), channel_id=1, replica_groups=mesh['sub'=8,'dom'=4] {'sub','dom'}, use_global_device_ids=true, to_apply=%region_29.33 | all-reduce | flops 2 | bytes 16 | tf_op jit(solution)/shard_map/psum | solution.py:112
  1265.4 42.0 %psum.62 = f32[]{:T(128)} all-reduce(f32[]{:T(128)} %get-tuple-element.336), channel_id=1, replica_groups=mesh['sub'=8,'dom'=4] {'sub','dom'}, use_global_device_ids=true, to_apply=%region_36.40 | all-reduce | flops 1 | bytes 8 | tf_op jit(solution)/shard_map/psum | solution.py:112
  1332.3 11.8 all-reduce.5
  1351.3 37.0 %psum.63 = f32[]{:T(128)} all-reduce(f32[]{:T(128)} %fusion.113), channel_id=1, replica_groups=mesh['sub'=8,'dom'=4] {'sub','dom'}, use_global_device_ids=true, to_apply=%region_41.45 | all-reduce | flops 1 | bytes 8 | tf_op jit(solution)/shard_map/psum | solution.py:112
  (573 shorter events, 354.5 us)
Async XLA Ops:
  8.3 18.8 %collective-permute-start = (f32[16,8,6,128]{3,1,2,0:T(8,128)S(1)}, f32[16,8,6,128]{3,1,2,0:T(8,128)S(1)}, u32[]{:S(2)}, u32[]{:S(2)}) collective-permute-start(f32[16,8,6,128]{3,1,2,0:T(8,128)S(1)} %all_gather.57), channel_id=1, source_target_pairs={{28,0},{0,4},{4,8},{8,12},{12,16},{16,20},{20,24},{24,28},{29,1},{... | collective-permute-start | bytes 1179656 | tf_op jit(solution)/shard_map/ppermute | solution.py:14
  9.8 19.5 %collective-permute-start.1 = (f32[16,8,6,128]{3,1,2,0:T(8,128)S(1)}, f32[16,8,6,128]{3,1,2,0:T(8,128)S(1)}, u32[]{:S(2)}, u32[]{:S(2)}) collective-permute-start(f32[16,8,6,128]{3,1,2,0:T(8,128)S(1)} %all_gather.57), channel_id=1, source_target_pairs={{4,0},{8,4},{12,8},{16,12},{20,16},{24,20},{28,24},{0,28},{5,1},{9... | collective-permute-start | bytes 1179656 | tf_op jit(solution)/shard_map/ppermute | solution.py:14
  485.7 4.9 collective-permute-start.2
  489.3 6.3 collective-permute-start.3
  495.6 7.3 collective-permute-start.5
  495.7 12.5 collective-permute-start.4
  527.1 4.1 collective-permute-start.6
  529.9 6.3 collective-permute-start.7
  619.5 10.2 collective-permute-start.8
  622.0 13.2 collective-permute-start.9
  655.0 6.3 collective-permute-start.11
  700.1 10.3 collective-permute-start.12
  702.6 13.4 collective-permute-start.13
  1178.3 3.7 collective-permute-start.14
  1178.4 6.4 collective-permute-start.15
  1184.8 10.0 collective-permute-start.16
  1184.8 15.2 %collective-permute-start.17 = (f32[6,4]{0,1:T(4,128)S(1)}, f32[6,4]{0,1:T(4,128)S(1)}, u32[]{:S(2)}, u32[]{:S(2)}) collective-permute-start(f32[6,4]{0,1:T(4,128)S(1)} %fusion.132), channel_id=1, source_target_pairs={{4,0},{8,4},{12,8},{16,12},{20,16},{24,20},{28,24},{0,28},{5,1},{9... | collective-permute-start | bytes 296 | tf_op jit(solution)/shard_map/ppermute | solution.py:14
  1219.2 3.6 collective-permute-start.18
  1219.2 6.3 collective-permute-start.19
  1308.7 10.2 collective-permute-start.20
  1311.2 13.2 collective-permute-start.21
  1344.2 6.3 collective-permute-start.23
  1389.7 10.3 collective-permute-start.24
  1392.3 13.3 collective-permute-start.25
  (8 other events, 561.4 us)
where the time goes:
time: 1410 us
  local copies, waits for them, and re-layouts  843 us (60%)
  blocking collectives  405 us (29%)
  other arithmetic  67 us (5%)
  starting transfers between devices  45.1 us (3%)
  waiting for transfers between devices  36.7 us (3%)
    gather x24, local copies, waits for them, and re-layouts, scan_terms(): chosen = jnp.take_along_axis(target_tiles, spread_lanes, axis=3)  732 us
    psum x6, blocking collectives, global_sum(): return lax.psum(value, ('sub', 'dom'))  232 us
    unnamed x6, blocking collectives  68.4 us
    gather x16, local copies, waits for them, and re-layouts, scan_terms(): picked = jnp.take(points, sources, axis=1)  46.4 us
    add x26, other arithmetic, rotate(): matrix[row_id, 0] * vector[0] + matrix[row_id, 1] * vector[1]  45.1 us
    ppermute x26, starting transfers between devices, from_behind(): return lax.ppermute(block, axis, route)  45.1 us
    ppermute x26, waiting for transfers between devices, from_behind(): return lax.ppermute(block, axis, route)  36.7 us
    all_gather x6, blocking collectives, spread_out(): lax.all_gather(pieces[0], 'dom', axis=1, tiled=True)  32.2 us
  transfers between devices with their start and end apart: 26, of which 14 were waited for; matrix products, arithmetic and copies ran while one was open for 1% of the time, Pallas kernels for 0%

commit v1 on v0

--- a/solution.py
+++ b/solution.py
@@ -109,7 +109,7 @@
 
 
 def global_sum(value):
-    return lax.psum(value, ("sub", "dom"))
+    return lax.psum(lax.psum(value, "dom"), "sub")
 
 
 def spread_out(own_part):

time: 1410 us -> 1330 us (0.943)
  blocking collectives: 405 us -> 316 us
    psum x6 -> x12, blocking collectives: 232 us -> 148 us  [global_sum(): return lax.psum(lax.psum(value, 'dom'), 'sub')]
where the time goes in v1:
time: 1330 us; the launch traced here: 1320 us
  local copies, waits for them, and re-layouts  843 us (63%)
  blocking collectives  316 us (24%)
  other arithmetic  66.8 us (5%)
  starting transfers between devices  45.1 us (3%)
  waiting for transfers between devices  36.7 us (3%)
    gather x24, local copies, waits for them, and re-layouts, scan_terms(): chosen = jnp.take_along_axis(target_tiles, spread_lanes, axis=3)  732 us
    psum x12, blocking collectives, global_sum(): return lax.psum(lax.psum(value, 'dom'), 'sub')  148 us
    unnamed x6, blocking collectives  66.2 us
    gather x16, local copies, waits for them, and re-layouts, scan_terms(): picked = jnp.take(points, sources, axis=1)  46.4 us
    add x26, other arithmetic, rotate(): matrix[row_id, 0] * vector[0] + matrix[row_id, 1] * vector[1]  45.1 us
    ppermute x26, starting transfers between devices, from_behind(): return lax.ppermute(block, axis, route)  45.1 us
    ppermute x26, waiting for transfers between devices, from_behind(): return lax.ppermute(block, axis, route)  36.7 us
    all_gather x6, blocking collectives, spread_out(): lax.all_gather(pieces[1], 'dom', axis=1, tiled=True)  31.3 us
  transfers between devices with their start and end apart: 26, of which 14 were waited for; matrix products, arithmetic and copies ran while one was open for 1% of the time, Pallas kernels for 0%

profile of v1, /device:TPU:0, one launch (start us, length us, event | category | flops | bytes accessed | tf_op | source)
XLA Modules:
  0.0 1323.5 jit_solution(17063593063039120895)
XLA Ops:
  0.0 8.3 all_gather.57
  31.0 440.6 %while.24 = (s32[]{:T(128)}, f32[4,4,6,6]{3,1,0,2:T(4,128)S(1)}, f32[4,4,6]{2,1,0:T(4,128)S(1)}, f32[4,12]{1,0:T(4,128)S(1)}, f32[4,3,4096]{1,2,0:T(8,128)}, /*i...) while((s32[]{:T(128)}, f32[4,4,6,6]{3,1,0,2:T(4,128)S(1)}, ...), condition=%wide.region_1.5_spmd, body=%wide.region_0.0_spmd.sunk | while | flops 1492314 | bytes 1967897 | solution.py:171
  47.1 91.5 %gather_fusion.1 = f32[12288]{0:T(1024)S(1)} fusion(f32[4,4,6,128]{3,2,1,0:T(8,128)S(1)} %bitcast.1328, s32[12288]{0:T(1024)S(1)} %reshape.2974), kind=kCustom, calls=%fused_computation.2.clone.clone.1 | custom fusion | bytes 294912 | tf_op jit(solution)/shard_map/while/body/eval_jaxpr/jit(take_along_axis)/gather | solution.py:78
  157.2 91.5 %gather_fusion.1 = f32[12288]{0:T(1024)S(1)} fusion(f32[4,4,6,128]{3,2,1,0:T(8,128)S(1)} %bitcast.1328, s32[12288]{0:T(1024)S(1)} %reshape.2974), kind=kCustom, calls=%fused_computation.2.clone.clone.1 | custom fusion | bytes 294912 | tf_op jit(solution)/shard_map/while/body/eval_jaxpr/jit(take_along_axis)/gather | solution.py:78
  267.4 91.5 %gather_fusion.1 = f32[12288]{0:T(1024)S(1)} fusion(f32[4,4,6,128]{3,2,1,0:T(8,128)S(1)} %bitcast.1328, s32[12288]{0:T(1024)S(1)} %reshape.2974), kind=kCustom, calls=%fused_computation.2.clone.clone.1 | custom fusion | bytes 294912 | tf_op jit(solution)/shard_map/while/body/eval_jaxpr/jit(take_along_axis)/gather | solution.py:78
  377.5 91.5 %gather_fusion.1 = f32[12288]{0:T(1024)S(1)} fusion(f32[4,4,6,128]{3,2,1,0:T(8,128)S(1)} %bitcast.1328, s32[12288]{0:T(1024)S(1)} %reshape.2974), kind=kCustom, calls=%fused_computation.2.clone.clone.1 | custom fusion | bytes 294912 | tf_op jit(solution)/shard_map/while/body/eval_jaxpr/jit(take_along_axis)/gather | solution.py:78
  475.1 10.5 all-reduce
  516.1 11.0 all-reduce.1
  536.9 6.3 all-reduce.9
  543.2 17.8 %all-reduce.7 = (f32[]{:T(128)}, f32[]{:T(128)}) all-reduce(f32[]{:T(128)} %get-tuple-element.310, f32[]{:T(128)} %get-tuple-element.311), channel_id=1, replica_groups=mesh['sub'=8,'dom'=4] {'sub'}, use_global_device_ids=true, to_apply=%region_9.13 | all-reduce | flops 2 | bytes 16 | tf_op jit(solution)/shard_map/psum | solution.py:112
  569.2 19.8 %psum.117 = f32[]{:T(128)} all-reduce(f32[]{:T(128)} %psum.116), channel_id=1, replica_groups=mesh['sub'=8,'dom'=4] {'sub'}, use_global_device_ids=true, to_apply=%region_18.22 | all-reduce | flops 1 | bytes 8 | tf_op jit(solution)/shard_map/psum | solution.py:112
  613.4 11.1 all-reduce.2
  637.8 17.7 %psum.119 = f32[]{:T(128)} all-reduce(f32[]{:T(128)} %psum.118), channel_id=1, replica_groups=mesh['sub'=8,'dom'=4] {'sub'}, use_global_device_ids=true, to_apply=%region_24.28 | all-reduce | flops 1 | bytes 8 | tf_op jit(solution)/shard_map/psum | solution.py:112
  678.3 440.6 %while.25 = (s32[]{:T(128)}, f32[4,4,6,6]{3,1,0,2:T(4,128)S(1)}, f32[4,4,6]{2,1,0:T(4,128)S(1)}, f32[4,12]{1,0:T(4,128)S(1)}, f32[4,3,4096]{1,2,0:T(8,128)}, /*i...) while((s32[]{:T(128)}, f32[4,4,6,6]{3,1,0,2:T(4,128)S(1)}, ...), condition=%wide.region_26.30_spmd, body=%wide.region_25.29_spmd.sunk | while | flops 1492314 | bytes 1967897 | solution.py:171
  694.3 91.5 %gather_fusion.5 = f32[12288]{0:T(1024)S(1)} fusion(f32[4,4,6,128]{3,2,1,0:T(8,128)S(1)} %bitcast.1329, s32[12288]{0:T(1024)S(1)} %reshape.2987), kind=kCustom, calls=%fused_computation.6.clone.clone.1 | custom fusion | bytes 294912 | tf_op jit(solution)/shard_map/while/body/eval_jaxpr/jit(take_along_axis)/gather | solution.py:78
  804.5 91.5 %gather_fusion.5 = f32[12288]{0:T(1024)S(1)} fusion(f32[4,4,6,128]{3,2,1,0:T(8,128)S(1)} %bitcast.1329, s32[12288]{0:T(1024)S(1)} %reshape.2987), kind=kCustom, calls=%fused_computation.6.clone.clone.1 | custom fusion | bytes 294912 | tf_op jit(solution)/shard_map/while/body/eval_jaxpr/jit(take_along_axis)/gather | solution.py:78
  914.6 91.5 %gather_fusion.5 = f32[12288]{0:T(1024)S(1)} fusion(f32[4,4,6,128]{3,2,1,0:T(8,128)S(1)} %bitcast.1329, s32[12288]{0:T(1024)S(1)} %reshape.2987), kind=kCustom, calls=%fused_computation.6.clone.clone.1 | custom fusion | bytes 294912 | tf_op jit(solution)/shard_map/while/body/eval_jaxpr/jit(take_along_axis)/gather | solution.py:78
  1024.8 91.5 %gather_fusion.5 = f32[12288]{0:T(1024)S(1)} fusion(f32[4,4,6,128]{3,2,1,0:T(8,128)S(1)} %bitcast.1329, s32[12288]{0:T(1024)S(1)} %reshape.2987), kind=kCustom, calls=%fused_computation.6.clone.clone.1 | custom fusion | bytes 294912 | tf_op jit(solution)/shard_map/while/body/eval_jaxpr/jit(take_along_axis)/gather | solution.py:78
  1122.4 11.4 all-reduce.3
  1163.4 11.1 all-reduce.4
  1188.0 17.8 %all-reduce.6 = (f32[]{:T(128)}, f32[]{:T(128)}) all-reduce(f32[]{:T(128)} %get-tuple-element.308, f32[]{:T(128)} %get-tuple-element.309), channel_id=1, replica_groups=mesh['sub'=8,'dom'=4] {'sub'}, use_global_device_ids=true, to_apply=%region_34.38 | all-reduce | flops 2 | bytes 16 | tf_op jit(solution)/shard_map/psum | solution.py:112
  1213.9 19.7 %psum.125 = f32[]{:T(128)} all-reduce(f32[]{:T(128)} %psum.124), channel_id=1, replica_groups=mesh['sub'=8,'dom'=4] {'sub'}, use_global_device_ids=true, to_apply=%region_43.47 | all-reduce | flops 1 | bytes 8 | tf_op jit(solution)/shard_map/psum | solution.py:112
  1258.1 11.0 all-reduce.5
  1282.6 17.8 %psum.127 = f32[]{:T(128)} all-reduce(f32[]{:T(128)} %psum.126), channel_id=1, replica_groups=mesh['sub'=8,'dom'=4] {'sub'}, use_global_device_ids=true, to_apply=%region_49.53 | all-reduce | flops 1 | bytes 8 | tf_op jit(solution)/shard_map/psum | solution.py:112
  (579 shorter events, 389.1 us)
Async XLA Ops:
  8.3 18.8 %collective-permute-start = (f32[16,8,6,128]{3,1,2,0:T(8,128)S(1)}, f32[16,8,6,128]{3,1,2,0:T(8,128)S(1)}, u32[]{:S(2)}, u32[]{:S(2)}) collective-permute-start(f32[16,8,6,128]{3,1,2,0:T(8,128)S(1)} %all_gather.57), channel_id=1, source_target_pairs={{28,0},{0,4},{4,8},{8,12},{12,16},{16,20},{20,24},{24,28},{29,1},{... | collective-permute-start | bytes 1179656 | tf_op jit(solution)/shard_map/ppermute | solution.py:14
  9.8 19.5 %collective-permute-start.1 = (f32[16,8,6,128]{3,1,2,0:T(8,128)S(1)}, f32[16,8,6,128]{3,1,2,0:T(8,128)S(1)}, u32[]{:S(2)}, u32[]{:S(2)}) collective-permute-start(f32[16,8,6,128]{3,1,2,0:T(8,128)S(1)} %all_gather.57), channel_id=1, source_target_pairs={{4,0},{8,4},{12,8},{16,12},{20,16},{24,20},{28,24},{0,28},{5,1},{9... | collective-permute-start | bytes 1179656 | tf_op jit(solution)/shard_map/ppermute | solution.py:14
  485.7 4.9 collective-permute-start.2
  489.3 6.3 collective-permute-start.3
  495.6 7.3 collective-permute-start.5
  495.7 12.5 collective-permute-start.4
  527.1 4.1 collective-permute-start.6
  529.9 6.3 collective-permute-start.7
  590.4 9.9 collective-permute-start.8
  590.4 15.1 %collective-permute-start.9 = (f32[6,4]{0,1:T(4,128)S(1)}, f32[6,4]{0,1:T(4,128)S(1)}, u32[]{:S(2)}, u32[]{:S(2)}) collective-permute-start(f32[6,4]{0,1:T(4,128)S(1)} %multiply_add_fusion.21), channel_id=1, source_target_pairs={{4,0},{8,4},{12,8},{16,12},{20,16},{24,20},{28,24},{0,28},{5,1},{9... | collective-permute-start | bytes 296 | tf_op jit(solution)/shard_map/ppermute | solution.py:14
  624.6 3.6 collective-permute-start.10
  624.6 6.3 collective-permute-start.11
  656.9 10.0 collective-permute-start.12
  658.9 13.2 %collective-permute-start.13 = (f32[6,4]{0,1:T(4,128)S(1)}, f32[6,4]{0,1:T(4,128)S(1)}, u32[]{:S(2)}, u32[]{:S(2)}) collective-permute-start(f32[6,4]{0,1:T(4,128)S(1)} %multiply_add_fusion.20), channel_id=1, source_target_pairs={{4,0},{8,4},{12,8},{16,12},{20,16},{24,20},{28,24},{0,28},{5,1},{9... | collective-permute-start | bytes 296 | tf_op jit(solution)/shard_map/ppermute | solution.py:14
  1133.8 3.7 collective-permute-start.14
  1133.9 6.4 collective-permute-start.15
  1140.3 10.0 collective-permute-start.16
  1140.3 15.2 %collective-permute-start.17 = (f32[6,4]{0,1:T(4,128)S(1)}, f32[6,4]{0,1:T(4,128)S(1)}, u32[]{:S(2)}, u32[]{:S(2)}) collective-permute-start(f32[6,4]{0,1:T(4,128)S(1)} %fusion.132), channel_id=1, source_target_pairs={{4,0},{8,4},{12,8},{16,12},{20,16},{24,20},{28,24},{0,28},{5,1},{9... | collective-permute-start | bytes 296 | tf_op jit(solution)/shard_map/ppermute | solution.py:14
  1174.6 6.3 collective-permute-start.19
  1235.0 9.9 collective-permute-start.20
  1235.0 15.1 %collective-permute-start.21 = (f32[6,4]{0,1:T(4,128)S(1)}, f32[6,4]{0,1:T(4,128)S(1)}, u32[]{:S(2)}, u32[]{:S(2)}) collective-permute-start(f32[6,4]{0,1:T(4,128)S(1)} %multiply_add_fusion.19), channel_id=1, source_target_pairs={{4,0},{8,4},{12,8},{16,12},{20,16},{24,20},{28,24},{0,28},{5,1},{9... | collective-permute-start | bytes 296 | tf_op jit(solution)/shard_map/ppermute | solution.py:14
  1269.2 6.3 collective-permute-start.23
  1301.9 10.0 collective-permute-start.24
  1303.9 13.2 %collective-permute-start.25 = (f32[6,4]{0,1:T(4,128)S(1)}, f32[6,4]{0,1:T(4,128)S(1)}, u32[]{:S(2)}, u32[]{:S(2)}) collective-permute-start(f32[6,4]{0,1:T(4,128)S(1)} %multiply_add_fusion.18), channel_id=1, source_target_pairs={{4,0},{8,4},{12,8},{16,12},{20,16},{24,20},{28,24},{0,28},{5,1},{9... | collective-permute-start | bytes 296 | tf_op jit(solution)/shard_map/ppermute | solution.py:14
  (8 other events, 561.4 us)
